TPU v7x, 32 devices: a whole 2x2x4 slice. The times are simulated.
32 devices in a mesh: groups: 2 (over y), expert: 16 (over z, x, core), tensor: 1.
Axes of the slice: x: 2, y: 2, z: 4, core: 2. Of those that a mesh axis runs over, the one named last changes fastest.
Arguments:
- tokens: bfloat16 [64, 4096], P(('groups', 'expert')), parts along dimension 0, may hold values from -6 to 6
- expert_ids: int32 [64, 2], P(('groups', 'expert')), parts along dimension 0, may hold values from 0 to 3, all different within a row; in each aligned block of 2 rows (0 to 1, 2 to 3, ...) at most 2 rows name the same one
- gate_weights: float32 [64, 2], P(('groups', 'expert')), parts along dimension 0, may hold values from 0.2 to 1
- doc_ids: int32 [64], P(('groups', 'expert')), parts along dimension 0, may hold values from 0 to 3, never falling along the last dimension, each value on 1 to 16 neighbouring positions
- w_gate: bfloat16 [4096, 2048], P(None, ('expert', 'tensor')), may hold values from -0.09375 to 0.09375
- w_up: bfloat16 [4096, 2048], P(None, ('expert', 'tensor')), may hold values from -0.09375 to 0.09375
- w_down: bfloat16 [2048, 4096], P(('expert', 'tensor')), may hold values from -0.25 to 0.25
- w_score: float32 [4096], P('tensor'), may hold values from -0.375 to 0.375
Outputs:
- mixed: bfloat16 [64, 4096], P(('groups', 'expert'), 'tensor'), parts along dimension 0
- scores: float32 [8], P('groups'), parts along dimension 0
There are 2 independent parts, one for each index of `groups`. A program takes and returns all parts, laid end to end along the dimension named above; an argument that names none is the same for every part. Nothing has to cross between parts.
Inputs may be any that keep to these rules, and one draw needn't show every extreme that they name: `expert_ids`: each row names two different experts. Among the rows of one device no expert is named more than 2 times, and in some devices' rows some expert exactly 2 times. `doc_ids`: document ids never fall along the tokens; every document holds 1 to 16 tokens, one exactly 16.
All inputs are finite; a program needn't handle non-finite values.
Results may differ from a plain program's by a relative error of at most 0.0057.
Values may be sent and summed in bfloat16 or wider, within the bound.
A program may use at most 64 MiB of HBM per device.

v0:
```python
import jax
import jax.numpy as jnp
from jax import lax
from jax.sharding import PartitionSpec as P

EXP_FLIGHT = 4
CAP = 2


def expert_block(rows, w_gate, w_up, w_down):
    shape_in = rows.shape
    flat = rows.reshape(-1, shape_in[-1])
    gate_part = jnp.dot(flat, w_gate, preferred_element_type=jnp.float32)
    up_part = jnp.dot(flat, w_up, preferred_element_type=jnp.float32)
    hidden = (jax.nn.silu(gate_part) * up_part).astype(jnp.bfloat16)
    partial_value = jnp.dot(hidden, w_down, preferred_element_type=jnp.float32).astype(jnp.bfloat16)
    partial_value = partial_value.reshape(shape_in)
    return lax.all_to_all(partial_value, "expert", split_axis=0, concat_axis=0, tiled=True)


def local(tokens, expert_ids, gate_weights, doc_ids, w_gate, w_up, w_down, w_score):
    expert_count = lax.axis_size("expert")
    tok_rows = tokens.shape[0]
    width = tokens.shape[1]
    spread = expert_count // EXP_FLIGHT
    slots_all = EXP_FLIGHT * CAP
    flat_ids = expert_ids.reshape(-1)
    picks = (flat_ids[:, None] == jnp.arange(EXP_FLIGHT, dtype=jnp.int32)[None, :]).astype(
        jnp.int32
    )
    earlier = jnp.cumsum(picks, axis=0) - picks
    slot_of = jnp.sum(earlier * picks, axis=1)
    target = flat_ids * CAP + slot_of
    places = jnp.arange(slots_all, dtype=jnp.int32)[:, None] == target[None, :]
    doubled = jnp.repeat(tokens, 2, axis=0)
    packed = jnp.dot(
        places.astype(jnp.bfloat16), doubled, preferred_element_type=jnp.float32
    ).astype(jnp.bfloat16)
    packed = packed.reshape(EXP_FLIGHT, 1, CAP, width)
    outgoing = jnp.broadcast_to(packed, (EXP_FLIGHT, spread, CAP, width)).reshape(
        expert_count, CAP, width
    )
    returned = expert_block(
        lax.all_to_all(outgoing, "expert", split_axis=0, concat_axis=0, tiled=True),
        w_gate,
        w_up,
        w_down,
    )
    summed = jnp.sum(returned.reshape(EXP_FLIGHT, spread, CAP, width), axis=1, dtype=jnp.float32)
    summed = summed.reshape(slots_all, width)
    weights_flat = gate_weights.reshape(-1)
    assign = jnp.where(places.T, weights_flat[:, None], jnp.float32(0.0))
    per_assign = jnp.dot(assign, summed, precision=lax.Precision.HIGHEST)
    mixed_part = jnp.sum(per_assign.reshape(tok_rows, 2, width), axis=1)
    mixed_wide = lax.psum_scatter(mixed_part, "tensor", scatter_dimension=1, tiled=True)
    mixed = mixed_wide.astype(jnp.bfloat16)
    projected = jnp.dot(mixed.astype(jnp.float32), w_score, precision=lax.Precision.HIGHEST)
    doc_total = tok_rows * expert_count // 8
    docs_hit = (doc_ids[:, None] == jnp.arange(doc_total, dtype=jnp.int32)[None, :]).astype(
        jnp.float32
    )
    doc_sums = jnp.dot(projected, docs_hit, precision=lax.Precision.HIGHEST)
    doc_counts = jnp.where(
        lax.axis_index("tensor") == 0, jnp.sum(docs_hit, axis=0), jnp.float32(0.0)
    )
    totals, counts = lax.psum((doc_sums, doc_counts), ("expert", "tensor"))
    scores = jax.nn.sigmoid(totals / counts)
    return (mixed, scores)


def solution(mesh):
    in_specs = (
        P(("groups", "expert"), None),
        P(("groups", "expert"), None),
        P(("groups", "expert"), None),
        P(("groups", "expert")),
        P(None, ("expert", "tensor")),
        P(None, ("expert", "tensor")),
        P(("expert", "tensor"), None),
        P("tensor"),
    )
    out_specs = (P(("groups", "expert"), "tensor"), P("groups"))
    return jax.shard_map(local, mesh=mesh, in_specs=in_specs, out_specs=out_specs, check_vma=False)
```

profile of v0, /device:TPU:0, one launch (start us, length us, event | category | flops | bytes accessed | tf_op | source)
XLA Modules:
  0.0 70.3 jit_solution(13723312300678550193)
XLA Ops:
  0.6 0.0 copy-start
  0.7 0.9 %eq.64 = s32[4]{0:T(128)S(1)} reshape(s32[2,2]{1,0:T(2,128)} %param.9) | data formatting | bytes 32 | tf_op jit(solution)/shard_map/eq | solution.py:28
  1.6 0.1 fusion.10
  1.7 0.2 select_reduce_fusion
  1.9 0.7 %broadcast_in_dim.31 = bf16[2,2,4096]{2,1,0:T(2,128)(2,1)S(1)} broadcast(bf16[2,4096]{1,0:T(2,128)(2,1)} %param.8), dimensions={0,2} | broadcast | bytes 49152 | tf_op jit(solution)/shard_map/broadcast_in_dim | solution.py:35
  2.6 0.1 convolution_convert_fusion.1
  2.8 0.1 broadcast_in_dim.32
  2.8 0.2 broadcast_in_dim.33
  3.1 17.3 %all_to_all.10 = bf16[16,2,4096]{2,1,0:T(2,128)(2,1)} all-to-all(bf16[16,2,4096]{2,1,0:T(2,128)(2,1)S(1)} %bitcast.23), channel_id=1, replica_groups=mesh['groups'=2,'expert'=16,'tensor'=1] {'expert'}, dimensions={0} | all-to-all | bytes 524288 | tf_op jit(solution)/shard_map/all_to_all | solution.py:44
  20.4 1.1 %reshape.70 = bf16[32,4096]{1,0:T(8,128)(2,1)S(1)} reshape(bf16[16,2,4096]{2,1,0:T(2,128)(2,1)} %all_to_all.10) | data formatting | bytes 524288 | tf_op jit(solution)/shard_map/reshape | solution.py:12
  21.5 0.3 fusion.18
  21.8 0.5 convolution_convert_fusion
  22.4 0.9 %reshape.71 = bf16[16,2,4096]{2,1,0:T(2,128)(2,1)} reshape(bf16[32,4096]{1,0:T(8,128)(2,1)S(1)} %convolution_convert_fusion) | data formatting | bytes 524288 | tf_op jit(solution)/shard_map/reshape | solution.py:17
  23.2 3.5 %all-to-all-start.1 = ((bf16[16,2,4096]{2,1,0:T(2,128)(2,1)}), bf16[16,2,4096]{2,1,0:T(2,128)(2,1)S(1)}, u32[]{:S(2)}, u32[]{:S(2)}) async-start(bf16[16,2,4096]{2,1,0:T(2,128)(2,1)} %reshape.71), calls=%async_computation.1 | async-start | bytes 524288 | tf_op jit(solution)/shard_map/all_to_all | solution.py:18
  26.8 0.0 copy-start.7
  26.8 0.1 reduce_sum.39
  26.9 0.6 copy-done.7
  27.4 0.1 convert_reduce_fusion.1
  27.5 0.6 copy-done.5
  28.1 8.6 %all-to-all-done.1 = bf16[16,2,4096]{2,1,0:T(2,128)(2,1)S(1)} async-done(((bf16[16,2,4096]{2,1,0:T(2,128)(2,1)}), bf16[16,2,4096]{2,1,0:T(2,128)(2,1)S(1)}, u32[]{:S(2)}, u32[]{:S(2)}) %all-to-all-start.1) | async-done | bytes 262176 | tf_op jit(solution)/shard_map/all_to_all | solution.py:18
  36.8 0.3 convert_reduce_fusion
  37.0 0.0 copy-start.4
  37.0 0.1 reshape.74
  37.1 0.6 copy-done.4
  37.7 0.4 convolution_reduce_fusion
  38.2 0.0 copy-start.3
  38.2 0.3 copy-done.6
  38.4 0.2 convolution_bitcast_fusion.1
  38.6 0.1 copy-done.3
  38.8 0.2 convolution_bitcast_fusion
  39.0 30.8 %all-reduce = (f32[4]{0:T(128)S(1)}, f32[4]{0:T(128)S(1)}) all-reduce(f32[4]{0:T(128)S(1)} %convolution_bitcast_fusion, f32[4]{0:T(128)S(1)} %convert_reduce_fusion.1), channel_id=1, replica_groups=mesh['groups'=2,'expert'=16,'tensor'=1] {'expert','tensor'}, use_global_device_ids=true, to_apply=%region_4.5 | all-reduce | flops 8 | bytes 64 | tf_op jit(solution)/shard_map/psum | solution.py:66
  69.7 0.5 add_divide_fusion
  (11 shorter events, 0.1 us)
Async XLA Ops:
  0.6 21.2 %copy-start = (bf16[128,4096]{1,0:T(8,128)(2,1)S(1)}, bf16[128,4096]{1,0:T(8,128)(2,1)}, u32[]{:S(2)}) copy-start(bf16[128,4096]{1,0:T(8,128)(2,1)} %param.14) | copy-start | bytes 3145732
  0.6 20.9 %copy-start.1 = (bf16[4096,128]{1,0:T(8,128)(2,1)S(1)}, bf16[4096,128]{1,0:T(8,128)(2,1)}, u32[]{:S(2)}) copy-start(bf16[4096,128]{1,0:T(8,128)(2,1)} %param.12) | copy-start | bytes 3145732
  20.4 1.5 %copy-start.2 = (bf16[4096,128]{1,0:T(8,128)(2,1)S(1)}, bf16[4096,128]{1,0:T(8,128)(2,1)}, u32[]{:S(2)}) copy-start(bf16[4096,128]{1,0:T(8,128)(2,1)} %param.13) | copy-start | bytes 3145732
  23.2 13.5 %all-to-all-start.1 = ((bf16[16,2,4096]{2,1,0:T(2,128)(2,1)}), bf16[16,2,4096]{2,1,0:T(2,128)(2,1)S(1)}, u32[]{:S(2)}, u32[]{:S(2)}) async-start(bf16[16,2,4096]{2,1,0:T(2,128)(2,1)} %reshape.71), calls=%async_computation.1 | async-start | bytes 524288 | tf_op jit(solution)/shard_map/all_to_all | solution.py:18
  26.8 0.7 copy-start.7
  27.4 0.7 copy-start.5
  37.0 0.7 copy-start.4
  37.7 0.7 %copy-start.6 = (f32[4096]{0:T(1024)S(1)}, f32[4096]{0:T(1024)}, u32[]{:S(2)}) copy-start(f32[4096]{0:T(1024)} %param.15) | copy-start | bytes 49156
  38.2 0.6 copy-start.3
where the time goes:
time: 70.8 us; the launch traced here: 70.3 us
  blocking collectives  48.1 us (68%)
  waiting for transfers between devices  8.64 us (12%)
  local copies, waits for them, and re-layouts  6.27 us (9%)
  starting transfers between devices  3.53 us (5%)
  matrix products  1.79 us (3%)
  other arithmetic  1.19 us (2%)
  between operations  0.77 us (1%)
    psum x1, blocking collectives, local(): totals, counts = lax.psum((doc_sums, doc_counts), ('expert', 'tensor'))  30.8 us
    all_to_all x1, blocking collectives, local(): lax.all_to_all(outgoing, 'expert', split_axis=0, concat_axis=0, tiled=True)  17.3 us
    all_to_all x1, waiting for transfers between devices, expert_block(): lax.all_to_all(partial_value, 'expert', split_axis=0, concat_axis=0, tile...  8.64 us
    all_to_all x1, starting transfers between devices, expert_block(): lax.all_to_all(partial_value, 'expert', split_axis=0, concat_axis=0, tile...  3.53 us
    unnamed x16, local copies, waits for them, and re-layouts  2.15 us
  transfers between devices with their start and end apart: 1, of which 1 were waited for; matrix products, arithmetic and copies ran while one was open for 0% of the time, Pallas kernels for 0%

commit v1 on v0

v1 whole, which is shorter than its diff:
```python
import functools

import jax
import jax.numpy as jnp
from jax import lax
from jax.experimental import pallas as pl
from jax.experimental.pallas import tpu as pltpu
from jax.sharding import PartitionSpec as P

EXP_FLIGHT = 4
LANES = 128
DOC_LANE = 64
MESH = pl.DeviceIdType.MESH
F32 = jnp.float32
BF16 = jnp.bfloat16


def is_pow2(n):
    return n & (n - 1) == 0


def partner(x, m, n):
    if not is_pow2(n):
        return lax.rem(x + m, n)
    out, bit = x, 1
    while bit < n:
        if m & bit:
            out = out + bit - 2 * bit * lax.rem(lax.div(x, bit), 2)
        bit *= 2
    return out


def source(x, m, n):
    return partner(x, m, n) if is_pow2(n) else lax.rem(x + n - m, n)


def three_parts(x):
    hi = x.astype(BF16).astype(F32)
    rest = x - hi
    mid = rest.astype(BF16).astype(F32)
    low = (rest - mid).astype(BF16).astype(F32)
    return hi, mid, low


def kernel(
    A, B, T, C, docs,
    tok_hbm, ids_hbm, gw_hbm, doc_hbm, wg_hbm, wu_hbm, wd_hbm, ws_hbm,
    mixed_ref, scores_ref,
    gathered, w1, w2, ws, ids, gw, doc,
    send1, recv1, send2, recv2, sums1, got1, sums2, got2,
    load_sem, z_send, z_recv, p_send, p_recv, r1_send, r1_recv, r2_send, r2_recv,
    s1_send, s1_recv, s2_send, s2_recv,
):
    rows, D = tok_hbm.shape
    hid = wg_hbm.shape[1]
    DT = D // T
    DC = DT // C
    Q = B * T
    me = lax.axis_index("expert")
    j = lax.axis_index("tensor")
    a, b = lax.div(me, B), lax.rem(me, B)
    q = b * T + j

    def z_peer(m):
        return {"expert": partner(a, m, A) * B + b, "tensor": j}

    def p_peer(m):
        return {"expert": a * B + partner(b, m, B), "tensor": j}

    def q_peer(m):
        to = partner(q, m, Q)
        return {"expert": a * B + lax.div(to, T), "tensor": lax.rem(to, T)}

    own = b * A + a
    loads = [
        pltpu.make_async_copy(tok_hbm, gathered.at[own, :, pl.ds(0, D)], load_sem.at[0]),
        pltpu.make_async_copy(ids_hbm, ids, load_sem.at[1]),
        pltpu.make_async_copy(gw_hbm, gw, load_sem.at[2]),
        pltpu.make_async_copy(doc_hbm, doc, load_sem.at[3]),
        pltpu.make_async_copy(wg_hbm, w1.at[:, pl.ds(0, hid)], load_sem.at[4]),
        pltpu.make_async_copy(wu_hbm, w1.at[:, pl.ds(hid, hid)], load_sem.at[5]),
        pltpu.make_async_copy(wd_hbm, w2, load_sem.at[6]),
        pltpu.make_async_copy(ws_hbm, ws, load_sem.at[7]),
    ]
    barrier = pltpu.get_barrier_semaphore()
    for m in range(1, A):
        pl.semaphore_signal(barrier, inc=1, device_id=z_peer(m), device_id_type=MESH)
    for m in range(1, Q):
        pl.semaphore_signal(barrier, inc=1, device_id=q_peer(m), device_id_type=MESH)
    for copy in loads:
        copy.start()

    for copy in loads[1:4]:
        copy.wait()
    lane = lax.broadcasted_iota(jnp.int32, (rows, LANES), 1)
    row = lax.broadcasted_iota(jnp.int32, (rows, LANES), 0)
    meta = jnp.zeros((rows, LANES), F32)
    for r in range(rows):
        for k in range(2):
            chosen, weight = ids[r, k], gw[r, k]
            for part, value in enumerate(three_parts(jnp.full((rows, LANES), weight, F32))):
                meta = jnp.where((row == r) & (lane == part * A + chosen), value, meta)
        meta = jnp.where((row == r) & (lane == DOC_LANE + doc[r]), F32(1.0), meta)
    gathered[own, :, pl.ds(D, LANES)] = meta.astype(BF16)
    loads[0].wait()
    pl.semaphore_wait(barrier, (A - 1) + (Q - 1))

    zs = {}
    for m in reversed(range(1, A)):
        zs[m] = pltpu.make_async_remote_copy(
            src_ref=gathered.at[own], dst_ref=gathered.at[own],
            send_sem=z_send.at[m - 1], recv_sem=z_recv.at[m - 1],
            device_id=z_peer(m), device_id_type=MESH,
        )
        zs[m].start()
    ps = []

    def forward(step):
        slot = b * A + source(a, step, A)
        for m in reversed(range(1, B)):
            at = step * (B - 1) + m - 1
            copy = pltpu.make_async_remote_copy(
                src_ref=gathered.at[slot], dst_ref=gathered.at[slot],
                send_sem=p_send.at[at], recv_sem=p_recv.at[at],
                device_id=p_peer(m), device_id_type=MESH,
            )
            copy.start()
            ps.append(copy)

    forward(0)
    loads[6].wait()
    loads[7].wait()
    hi, mid, low = three_parts(ws[...])
    srow = lax.broadcasted_iota(jnp.int32, (16, D), 0)
    left = jnp.where(srow == 0, hi, jnp.where(srow == 1, mid, jnp.where(srow == 2, low, 0.0)))
    seen = lax.dot_general(
        left.astype(BF16), w2[...], (((1,), (1,)), ((), ())), preferred_element_type=F32
    )
    seen = jnp.sum(seen, axis=0, keepdims=True)
    loads[4].wait()
    loads[5].wait()
    for m in range(1, A):
        zs[m].wait_recv()
        forward(m)
    for copy in ps:
        copy.wait_recv()

    n_tok = A * B * rows
    everyone = gathered[...].reshape(n_tok, D + LANES)
    x = everyone[:, :D]
    meta = everyone[:, D:].astype(F32)
    lane = lax.broadcasted_iota(jnp.int32, (n_tok, LANES), 1)
    mine = (lane < 3 * A) & (lax.rem(lane, A) == a)
    weight = jnp.sum(jnp.where(mine, meta, 0.0), axis=1, keepdims=True)
    hits = jnp.where(lane >= DOC_LANE, meta, 0.0)
    both = jnp.dot(x, w1[...], preferred_element_type=F32)
    gate, up = both[:, :hid], both[:, hid:]
    hidden = ((gate / (1.0 + jnp.exp(-gate))) * up).astype(BF16)

    firsts = []
    for c in range(C):
        for t in range(T):
            part = jnp.dot(
                hidden, w2[:, t * DT + c * DC:t * DT + (c + 1) * DC], preferred_element_type=F32
            )
            part = (part * weight).reshape(B, A * rows, DC)
            send1[t, :, :, c * DC:(c + 1) * DC] = part.astype(BF16)
        for m in reversed(range(1, Q)):
            to = partner(q, m, Q)
            at = c * (Q - 1) + m - 1
            copy = pltpu.make_async_remote_copy(
                src_ref=send1.at[lax.rem(to, T), lax.div(to, T), :, pl.ds(c * DC, DC)],
                dst_ref=recv1.at[m - 1, :, pl.ds(c * DC, DC)],
                send_sem=r1_send.at[at], recv_sem=r1_recv.at[at],
                device_id=q_peer(m), device_id_type=MESH,
            )
            copy.start()
            firsts.append((c, copy))
    seen_by = jnp.sum(hidden.astype(F32) * seen, axis=1, keepdims=True) * weight
    sums = jnp.sum(hits * seen_by, axis=0, keepdims=True)
    counts = jnp.sum(hits, axis=0, keepdims=True)
    sums1[...] = jnp.broadcast_to(sums, (8, LANES))
    s_first = []
    for m in range(1, Q):
        copy = pltpu.make_async_remote_copy(
            src_ref=sums1, dst_ref=got1.at[m - 1],
            send_sem=s1_send.at[m - 1], recv_sem=s1_recv.at[m - 1],
            device_id=q_peer(m), device_id_type=MESH,
        )
        copy.start()
        s_first.append(copy)

    seconds = []
    for c in range(C):
        for at, copy in firsts:
            if at == c:
                copy.wait_recv()
        cols = pl.ds(c * DC, DC)
        total = send1[j, b, :, cols].astype(F32)
        for m in range(1, Q):
            total = total + recv1[m - 1, :, cols].astype(F32)
        for to in range(A):
            send2[to, :, cols] = total[to * rows:(to + 1) * rows].astype(BF16)
        for m in reversed(range(1, A)):
            at = c * (A - 1) + m - 1
            copy = pltpu.make_async_remote_copy(
                src_ref=send2.at[partner(a, m, A), :, cols],
                dst_ref=recv2.at[m - 1, :, cols],
                send_sem=r2_send.at[at], recv_sem=r2_recv.at[at],
                device_id=z_peer(m), device_id_type=MESH,
            )
            copy.start()
            seconds.append((c, copy))
    for copy in s_first:
        copy.wait_recv()
    plane = sums1[...]
    for m in range(1, Q):
        plane = plane + got1[m - 1]
    sums2[...] = plane
    s_second = []
    for m in reversed(range(1, A)):
        copy = pltpu.make_async_remote_copy(
            src_ref=sums2, dst_ref=got2.at[m - 1],
            send_sem=s2_send.at[m - 1], recv_sem=s2_recv.at[m - 1],
            device_id=z_peer(m), device_id_type=MESH,
        )
        copy.start()
        s_second.append(copy)

    for c in range(C):
        for at, copy in seconds:
            if at == c:
                copy.wait_recv()
        cols = pl.ds(c * DC, DC)
        total = send2[a, :, cols].astype(F32)
        for m in range(1, A):
            total = total + recv2[m - 1, :, cols].astype(F32)
        mixed_ref[:, cols] = total.astype(BF16)
    for copy in s_second:
        copy.wait_recv()
    totals = sums2[...]
    for m in range(1, A):
        totals = totals + got2[m - 1]
    mean = totals[0:1, DOC_LANE:DOC_LANE + docs] / counts[:, DOC_LANE:DOC_LANE + docs]
    scores_ref[...] = 1.0 / (1.0 + jnp.exp(-mean))

    for copy in list(zs.values()) + ps + [c for _, c in firsts] + s_first:
        copy.wait_send()
    for copy in [c for _, c in seconds] + s_second:
        copy.wait_send()


def solution(mesh):
    E, T = mesh.shape["expert"], mesh.shape["tensor"]
    A = EXP_FLIGHT
    B = E // A
    Q = B * T

    def local(tokens, expert_ids, gate_weights, doc_ids, w_gate, w_up, w_down, w_score):
        rows, D = tokens.shape
        hid = w_gate.shape[1]
        docs = rows * E // 8
        assert 3 * A <= DOC_LANE and DOC_LANE + docs <= LANES
        DT = D // T
        C = next(c for c in (4, 2, 1) if DT % (c * LANES) == 0)
        if T > 1:
            w_score = lax.all_gather(w_score, "tensor", tiled=True)
        dma = pltpu.SemaphoreType.DMA
        any_spec = pl.BlockSpec(memory_space=pl.ANY)
        mixed, scores = pl.pallas_call(
            functools.partial(kernel, A, B, T, C, docs),
            out_shape=(
                jax.ShapeDtypeStruct((rows, DT), BF16),
                jax.ShapeDtypeStruct((1, docs), F32),
            ),
            in_specs=[any_spec] * 8,
            out_specs=(
                pl.BlockSpec(memory_space=pltpu.VMEM),
                pl.BlockSpec(memory_space=pltpu.VMEM),
            ),
            scratch_shapes=[
                pltpu.VMEM((E, rows, D + LANES), BF16),
                pltpu.VMEM((D, 2 * hid), BF16),
                pltpu.VMEM((hid, D), BF16),
                pltpu.VMEM((1, D), F32),
                pltpu.SMEM(expert_ids.shape, jnp.int32),
                pltpu.SMEM(gate_weights.shape, F32),
                pltpu.SMEM(doc_ids.shape, jnp.int32),
                pltpu.VMEM((T, B, A * rows, DT), BF16),
                pltpu.VMEM((Q - 1, A * rows, DT), BF16),
                pltpu.VMEM((A, rows, DT), BF16),
                pltpu.VMEM((A - 1, rows, DT), BF16),
                pltpu.VMEM((8, LANES), F32),
                pltpu.VMEM((Q - 1, 8, LANES), F32),
                pltpu.VMEM((8, LANES), F32),
                pltpu.VMEM((A - 1, 8, LANES), F32),
                dma((8,)),
                dma((A - 1,)), dma((A - 1,)),
                dma((A * (B - 1),)), dma((A * (B - 1),)),
                dma((C * (Q - 1),)), dma((C * (Q - 1),)),
                dma((C * (A - 1),)), dma((C * (A - 1),)),
                dma((Q - 1,)), dma((Q - 1,)),
                dma((A - 1,)), dma((A - 1,)),
            ],
            compiler_params=pltpu.CompilerParams(collective_id=0, has_side_effects=True),
        )(
            tokens, expert_ids, gate_weights, doc_ids, w_gate, w_up, w_down,
            w_score.reshape(1, D),
        )
        return mixed, scores.reshape(docs)

    in_specs = (
        P(("groups", "expert"), None),
        P(("groups", "expert"), None),
        P(("groups", "expert"), None),
        P(("groups", "expert")),
        P(None, ("expert", "tensor")),
        P(None, ("expert", "tensor")),
        P(("expert", "tensor"), None),
        P("tensor"),
    )
    out_specs = (P(("groups", "expert"), "tensor"), P("groups"))
    return jax.shard_map(local, mesh=mesh, in_specs=in_specs, out_specs=out_specs, check_vma=False)
```

time: 70.8 us -> 24.9 us (0.35)
  blocking collectives: 48.1 us -> 0 us
  Pallas kernels: 0 us -> 22.2 us
  waiting for transfers between devices: 8.64 us -> 0 us
  local copies, waits for them, and re-layouts: 6.27 us -> 1.85 us
  starting transfers between devices: 3.53 us -> 0 us
  matrix products: 1.79 us -> 0 us
  other arithmetic: 1.19 us -> 0 us
    psum x1 -> x0, blocking collectives: 30.8 us -> none  [local(): totals, counts = lax.psum((doc_sums, doc_counts), ('expert', 'tensor'))]
    pallas_call x0 -> x1, Pallas kernels: none -> 22.2 us  [local(): pl.pallas_call(functools.partial(kernel, A, B, T, C, docs), out_shape=(ja...]
    all_to_all x1 -> x0, blocking collectives: 17.3 us -> none  [local(): lax.all_to_all(outgoing, 'expert', split_axis=0, concat_axis=0, tiled=True)]
    all_to_all x1 -> x0, waiting for transfers between devices: 8.64 us -> none  [expert_block(): lax.all_to_all(partial_value, 'expert', split_axis=0, concat_axis=0, tile...]
    all_to_all x1 -> x0, starting transfers between devices: 3.53 us -> none  [expert_block(): lax.all_to_all(partial_value, 'expert', split_axis=0, concat_axis=0, tile...]
    reshape x4 -> x0, local copies, waits for them, and re-layouts: 2.13 us -> none  [the longest x1 1.14 us: expert_block(): flat = rows.reshape(-1, shape_in[-1])]
    dot_general x6 -> x0, matrix products: 1.79 us -> none  [the longest x1 0.53 us: expert_block(): jnp.dot(hidden, w_down, preferred_element_type=jnp.float32)]
    broadcast_in_dim x3 -> x0, local copies, waits for them, and re-layouts: 1 us -> none  [the longest x1 0.74 us: local(): doubled = jnp.repeat(tokens, 2, axis=0)]
  transfers between devices with their start and end apart: 1 -> 0, of which waited for: 1 -> 0; matrix products, arithmetic and copies ran while one was open for 0% -> 0% of each run, Pallas kernels for 0% -> 0%
where the time goes in v1:
time: 24.9 us; the launch traced here: 24.7 us
  Pallas kernels  22.2 us (89%)
  local copies, waits for them, and re-layouts  1.85 us (7%)
  between operations  0.65 us (3%)
    pallas_call x1, Pallas kernels, local(): pl.pallas_call(functools.partial(kernel, A, B, T, C, docs), out_shape=(ja...  22.2 us
    unnamed x4, local copies, waits for them, and re-layouts  1.85 us

profile of v1, /device:TPU:0, one launch (start us, length us, event | category | flops | bytes accessed | tf_op | source)
XLA Modules:
  0.0 24.7 jit_solution(866252851843195278)
XLA Ops:
  0.6 22.2 %shard_map.95 = (bf16[2,4096]{1,0:T(2,128)(2,1)}, f32[1,4]{1,0:T(1,128)}) custom-call(bf16[2,4096]{1,0:T(2,128)(2,1)} %tok_hbm.1, s32[2,2]{1,0:T(2,128)} %ids_hbm.1, f32[2,2]{1,0:T(2,128)} %gw_hbm.1, s32[2]{0:T(128)} %doc_hbm.1, bf16[4096,128]{1,0:T(8,128)(2,1)} %wg_hbm.1, bf16[4096,128]{1,0:T(8,128)(2,1)} %wu_hbm.1, bf16[128,4096]{1,0:T(8,128)(2,1)} %wd_hbm.1, ...), custom_call_target="tpu_custom_call" | custom-call | tf_op jit(solution)/shard_map/pallas_call | solution.py:270
  22.8 0.0 copy-start
  22.8 1.3 %copy.12 = bf16[2,4096]{1,0:T(2,128)(2,1)} copy(bf16[2,4096]{1,0:T(2,128)(2,1)} %get-tuple-element.8) | data formatting | bytes 32768
  24.2 0.0 copy-done
  24.2 0.5 %copy.13 = f32[4]{0:T(128)} copy(f32[4]{0:T(128)S(1)} %bitcast.3) | data formatting | bytes 32
Async XLA Ops:
  22.8 1.3 %copy-start = (f32[1,4]{1,0:T(1,128)S(1)}, f32[1,4]{1,0:T(1,128)}, u32[]{:S(2)}) copy-start(f32[1,4]{1,0:T(1,128)} %get-tuple-element.5) | copy-start | bytes 52

commit v2 on v1

v2 whole, which is shorter than its diff:
```python
import functools

import jax
import jax.numpy as jnp
from jax import lax
from jax.experimental import pallas as pl
from jax.experimental.pallas import tpu as pltpu
from jax.sharding import PartitionSpec as P

EXP_FLIGHT = 4
CORES = 2
CHUNKS = 2
LANES = 128
DOC_LANE = 64
MESH = pl.DeviceIdType.MESH
F32 = jnp.float32
BF16 = jnp.bfloat16


def is_pow2(n):
    return n & (n - 1) == 0


def partner(x, m, n):
    if not is_pow2(n):
        return lax.rem(x + m, n)
    out, bit = x, 1
    while bit < n:
        if m & bit:
            out = out + bit - 2 * bit * lax.rem(lax.div(x, bit), 2)
        bit *= 2
    return out


def source(x, m, n):
    return partner(x, m, n) if is_pow2(n) else lax.rem(x + n - m, n)


def three_parts(x):
    hi = x.astype(BF16).astype(F32)
    rest = x - hi
    mid = rest.astype(BF16).astype(F32)
    low = (rest - mid).astype(BF16).astype(F32)
    return hi, mid, low


def kernel(
    spread, L, T, C, docs,
    tok_hbm, ids_hbm, gw_hbm, doc_hbm, wg_hbm, wu_hbm, wd_hbm, ws_hbm,
    mixed_ref, scores_ref,
    gathered, w1, w2, ws, ids, gw, doc,
    send1, recv1, kept, send2, recv2, sums1, got1, sums2, got2,
    load_sem, g_send, g_recv, p_send, p_recv, r1_send, r1_recv, r2_send, r2_recv,
    s1_send, s1_recv, s2_send, s2_recv,
):
    rows, D = tok_hbm.shape
    hid = wg_hbm.shape[1]
    DT = D // T
    DC = DT // C
    A = EXP_FLIGHT
    slots = gathered.shape[0]
    me = lax.axis_index("expert")
    j = lax.axis_index("tensor")
    flat = me * T + j
    core, chip = lax.rem(flat, CORES), lax.div(flat, CORES)
    expert = lax.div(me, spread)

    def device(core, chip):
        to = chip * CORES + core
        return {"expert": lax.div(to, T), "tensor": lax.rem(to, T)}

    def line_peer(m):
        return device(core, partner(chip, m, L))

    other_core = device(1 - core, chip)

    def slot_of(core, chip):
        return core * L + chip if T == 1 else chip

    own = slot_of(core, chip)
    loads = [
        pltpu.make_async_copy(tok_hbm, gathered.at[own, :, pl.ds(0, D)], load_sem.at[0]),
        pltpu.make_async_copy(ids_hbm, ids, load_sem.at[1]),
        pltpu.make_async_copy(gw_hbm, gw, load_sem.at[2]),
        pltpu.make_async_copy(doc_hbm, doc, load_sem.at[3]),
        pltpu.make_async_copy(wg_hbm, w1.at[:, pl.ds(0, hid)], load_sem.at[4]),
        pltpu.make_async_copy(wu_hbm, w1.at[:, pl.ds(hid, hid)], load_sem.at[5]),
        pltpu.make_async_copy(wd_hbm, w2, load_sem.at[6]),
        pltpu.make_async_copy(ws_hbm, ws, load_sem.at[7]),
    ]
    barrier = pltpu.get_barrier_semaphore()
    for m in reversed(range(1, L)):
        pl.semaphore_signal(barrier, inc=1, device_id=line_peer(m), device_id_type=MESH)
    pl.semaphore_signal(barrier, inc=1, device_id=other_core, device_id_type=MESH)
    for copy in loads:
        copy.start()

    for copy in loads[1:4]:
        copy.wait()
    lane = lax.broadcasted_iota(jnp.int32, (rows, LANES), 1)
    row = lax.broadcasted_iota(jnp.int32, (rows, LANES), 0)
    meta = jnp.zeros((rows, LANES), F32)
    for r in range(rows):
        for k in range(2):
            chosen, weight = ids[r, k], gw[r, k]
            for part, value in enumerate(three_parts(jnp.full((rows, LANES), weight, F32))):
                meta = jnp.where((row == r) & (lane == part * A + chosen), value, meta)
        meta = jnp.where((row == r) & (lane == DOC_LANE + doc[r]), F32(1.0), meta)
    gathered[own, :, pl.ds(D, LANES)] = meta.astype(BF16)
    loads[0].wait()
    pl.semaphore_wait(barrier, L)

    straight = {}
    for m in reversed(range(1, L)):
        straight[m] = pltpu.make_async_remote_copy(
            src_ref=gathered.at[own], dst_ref=gathered.at[own],
            send_sem=g_send.at[m - 1], recv_sem=g_recv.at[m - 1],
            device_id=line_peer(m), device_id_type=MESH,
        )
        straight[m].start()
    passed = []

    def forward(m):
        slot = slot_of(core, source(chip, m, L))
        copy = pltpu.make_async_remote_copy(
            src_ref=gathered.at[slot], dst_ref=gathered.at[slot],
            send_sem=p_send.at[m], recv_sem=p_recv.at[m],
            device_id=other_core, device_id_type=MESH,
        )
        copy.start()
        passed.append(copy)

    if T == 1:
        forward(0)
    loads[6].wait()
    loads[7].wait()
    hi, mid, low = three_parts(ws[...])
    srow = lax.broadcasted_iota(jnp.int32, (16, D), 0)
    left = jnp.where(srow == 0, hi, jnp.where(srow == 1, mid, jnp.where(srow == 2, low, 0.0)))
    seen = lax.dot_general(
        left.astype(BF16), w2[...], (((1,), (1,)), ((), ())), preferred_element_type=F32
    )
    seen = jnp.sum(seen, axis=0, keepdims=True)
    loads[4].wait()
    loads[5].wait()
    for m in range(1, L):
        straight[m].wait_recv()
        if T == 1:
            forward(m)
    for copy in passed:
        copy.wait_recv()

    n_tok = slots * rows
    everyone = gathered[...].reshape(n_tok, D + LANES)
    x = everyone[:, :D]
    meta = everyone[:, D:].astype(F32)
    lane = lax.broadcasted_iota(jnp.int32, (n_tok, LANES), 1)
    mine = (lane < 3 * A) & (lax.rem(lane, A) == expert)
    weight = jnp.sum(jnp.where(mine, meta, 0.0), axis=1, keepdims=True)
    hits = jnp.where(lane >= DOC_LANE, meta, 0.0)
    both = jnp.dot(x, w1[...], preferred_element_type=F32)
    gate, up = both[:, :hid], both[:, hid:]
    hidden = ((gate / (1.0 + jnp.exp(-gate))) * up).astype(BF16)

    firsts = []
    for c in range(C):
        if T == 1:
            part = jnp.dot(hidden, w2[:, c * DC:(c + 1) * DC], preferred_element_type=F32) * weight
            low_half, high_half = part[:L * rows], part[L * rows:]
        else:
            low_half, high_half = (
                jnp.dot(
                    hidden, w2[:, h * DT + c * DC:h * DT + (c + 1) * DC],
                    preferred_element_type=F32,
                ) * weight
                for h in range(CORES)
            )
        cols = pl.ds(c * DC, DC)
        send1[:, cols] = jnp.where(core == 0, high_half, low_half).astype(BF16)
        copy = pltpu.make_async_remote_copy(
            src_ref=send1.at[:, cols], dst_ref=recv1.at[:, cols],
            send_sem=r1_send.at[c], recv_sem=r1_recv.at[c],
            device_id=other_core, device_id_type=MESH,
        )
        copy.start()
        firsts.append(copy)
        kept[:, cols] = jnp.where(core == 0, low_half, high_half)
    seen_by = jnp.sum(hidden.astype(F32) * seen, axis=1, keepdims=True) * weight
    sums1[...] = jnp.sum(hits * seen_by, axis=0, keepdims=True)
    counts = jnp.sum(hits, axis=0, keepdims=True)
    s_first = pltpu.make_async_remote_copy(
        src_ref=sums1, dst_ref=got1, send_sem=s1_send.at[0], recv_sem=s1_recv.at[0],
        device_id=other_core, device_id_type=MESH,
    )
    s_first.start()

    seconds = []
    for c in range(C):
        firsts[c].wait_recv()
        cols = pl.ds(c * DC, DC)
        total = kept[:, cols] + recv1[:, cols].astype(F32)
        for to in range(L):
            send2[to, :, cols] = total[to * rows:(to + 1) * rows].astype(BF16)
        for m in reversed(range(1, L)):
            at = c * (L - 1) + m - 1
            copy = pltpu.make_async_remote_copy(
                src_ref=send2.at[partner(chip, m, L), :, cols],
                dst_ref=recv2.at[m - 1, :, cols],
                send_sem=r2_send.at[at], recv_sem=r2_recv.at[at],
                device_id=line_peer(m), device_id_type=MESH,
            )
            copy.start()
            seconds.append((c, copy))
        if c == 0:
            s_first.wait_recv()
            sums2[...] = sums1[...] + got1[...]
            s_second = []
            for m in reversed(range(1, L)):
                copy = pltpu.make_async_remote_copy(
                    src_ref=sums2, dst_ref=got2.at[m - 1],
                    send_sem=s2_send.at[m - 1], recv_sem=s2_recv.at[m - 1],
                    device_id=line_peer(m), device_id_type=MESH,
                )
                copy.start()
                s_second.append(copy)

    for copy in s_second:
        copy.wait_recv()
    totals = sums2[...]
    for m in range(1, L):
        totals = totals + got2[m - 1]
    docs_at = slice(DOC_LANE, DOC_LANE + docs)
    mean = totals[:, docs_at] / counts[:, docs_at]
    scores_ref[...] = 1.0 / (1.0 + jnp.exp(-mean))
    for c in range(C):
        for at, copy in seconds:
            if at == c:
                copy.wait_recv()
        cols = pl.ds(c * DC, DC)
        total = send2[chip, :, cols].astype(F32)
        for m in range(1, L):
            total = total + recv2[m - 1, :, cols].astype(F32)
        mixed_ref[:, cols] = total.astype(BF16)

    for copy in list(straight.values()) + passed + firsts + [s_first]:
        copy.wait_send()
    for copy in [c for _, c in seconds] + s_second:
        copy.wait_send()


def solution(mesh):
    E, T = mesh.shape["expert"], mesh.shape["tensor"]
    assert T in (1, CORES) and E * T % CORES == 0
    L = E * T // CORES

    def local(tokens, expert_ids, gate_weights, doc_ids, w_gate, w_up, w_down, w_score):
        rows, D = tokens.shape
        hid = w_gate.shape[1]
        docs = rows * E // 8
        assert 3 * EXP_FLIGHT <= DOC_LANE and DOC_LANE + docs <= LANES
        DT = D // T
        C = next(c for c in (CHUNKS, 1) if DT % (c * LANES) == 0)
        if T > 1:
            w_score = lax.all_gather(w_score, "tensor", tiled=True)
        dma = pltpu.SemaphoreType.DMA
        any_spec = pl.BlockSpec(memory_space=pl.ANY)
        mixed, scores = pl.pallas_call(
            functools.partial(kernel, E // EXP_FLIGHT, L, T, C, docs),
            out_shape=(
                pltpu.VMEM((rows, DT), BF16),
                pltpu.VMEM((1, docs), F32),
            ),
            in_specs=[any_spec] * 8,
            out_specs=(
                pl.BlockSpec(memory_space=pltpu.VMEM),
                pl.BlockSpec(memory_space=pltpu.VMEM),
            ),
            scratch_shapes=[
                pltpu.VMEM((E, rows, D + LANES), BF16),
                pltpu.VMEM((D, 2 * hid), BF16),
                pltpu.VMEM((hid, D), BF16),
                pltpu.VMEM((1, D), F32),
                pltpu.SMEM(expert_ids.shape, jnp.int32),
                pltpu.SMEM(gate_weights.shape, F32),
                pltpu.SMEM(doc_ids.shape, jnp.int32),
                pltpu.VMEM((L * rows, DT), BF16),
                pltpu.VMEM((L * rows, DT), BF16),
                pltpu.VMEM((L * rows, DT), F32),
                pltpu.VMEM((L, rows, DT), BF16),
                pltpu.VMEM((L - 1, rows, DT), BF16),
                pltpu.VMEM((1, LANES), F32),
                pltpu.VMEM((1, LANES), F32),
                pltpu.VMEM((1, LANES), F32),
                pltpu.VMEM((L - 1, 1, LANES), F32),
                dma((8,)),
                dma((L - 1,)), dma((L - 1,)),
                dma((L,)), dma((L,)),
                dma((C,)), dma((C,)),
                dma((C * (L - 1),)), dma((C * (L - 1),)),
                dma((1,)), dma((1,)),
                dma((L - 1,)), dma((L - 1,)),
            ],
            compiler_params=pltpu.CompilerParams(collective_id=0, has_side_effects=True),
        )(
            tokens, expert_ids, gate_weights, doc_ids, w_gate, w_up, w_down,
            w_score.reshape(1, D),
        )
        return mixed, scores.reshape(docs)

    in_specs = (
        P(("groups", "expert"), None),
        P(("groups", "expert"), None),
        P(("groups", "expert"), None),
        P(("groups", "expert")),
        P(None, ("expert", "tensor")),
        P(None, ("expert", "tensor")),
        P(("expert", "tensor"), None),
        P("tensor"),
    )
    out_specs = (P(("groups", "expert"), "tensor"), P("groups"))
    return jax.shard_map(local, mesh=mesh, in_specs=in_specs, out_specs=out_specs, check_vma=False)
```

time: 24.9 us -> 21 us (0.84)
  Pallas kernels: 22.2 us -> 19.1 us
  local copies, waits for them, and re-layouts: 1.85 us -> 1.12 us
    pallas_call x1, Pallas kernels: 22.2 us -> 19.1 us  [local(): pl.pallas_call(functools.partial(kernel, E // EXP_FLIGHT, L, T, C, docs),...]
    unnamed x4 -> x2, local copies, waits for them, and re-layouts: 1.85 us -> 1.12 us
where the time goes in v2:
time: 21 us; the launch traced here: 20.9 us
  Pallas kernels  19.1 us (91%)
  local copies, waits for them, and re-layouts  1.12 us (5%)
  between operations  0.64 us (3%)
    pallas_call x1, Pallas kernels, local(): pl.pallas_call(functools.partial(kernel, E // EXP_FLIGHT, L, T, C, docs),...  19.1 us
    unnamed x2, local copies, waits for them, and re-layouts  1.12 us

profile of v2, /device:TPU:0, one launch (start us, length us, event | category | flops | bytes accessed | tf_op | source)
XLA Modules:
  0.0 20.9 jit_solution(11612203954700438257)
XLA Ops:
  0.6 19.1 %shard_map.95 = (bf16[2,4096]{1,0:T(2,128)(2,1)S(1)}, f32[1,4]{1,0:T(1,128)S(1)}) custom-call(bf16[2,4096]{1,0:T(2,128)(2,1)} %tok_hbm.1, s32[2,2]{1,0:T(2,128)} %ids_hbm.1, f32[2,2]{1,0:T(2,128)} %gw_hbm.1, s32[2]{0:T(128)} %doc_hbm.1, bf16[4096,128]{1,0:T(8,128)(2,1)} %wg_hbm.1, bf16[4096,128]{1,0:T(8,128)(2,1)} %wu_hbm.1, bf16[128,4096]{1,0:T(8,128)(2,1)} %wd_hbm.1, ...), custom_call_target="tpu_custom_call" | custom-call | tf_op jit(solution)/shard_map/pallas_call | solution.py:267
  19.7 0.6 %copy.12 = bf16[2,4096]{1,0:T(2,128)(2,1)} copy(bf16[2,4096]{1,0:T(2,128)(2,1)S(1)} %get-tuple-element.6) | data formatting | bytes 32768
  20.4 0.5 %copy.13 = f32[4]{0:T(128)} copy(f32[4]{0:T(128)S(1)} %bitcast.2) | data formatting | bytes 32
